TPU v7x, 32 devices: a whole 2x2x4 slice. The times are simulated.
32 devices in a mesh: snap: 2 (over y), row: 8 (over z, x), col: 2 (over core).
Axes of the slice: x: 2, y: 2, z: 4, core: 2. Of those that a mesh axis runs over, the one named last changes fastest.
Arguments:
- density: bfloat16 [8192, 1024], P(('snap', 'row'), 'col'), parts along dimension 0, may hold values from -0.5 to 2
- pattern: int32 [256, 32], P(('snap', 'row'), 'col'), parts along dimension 0, may hold values 0 or 1
- filter_mask: int32 [256, 32], P(('snap', 'row')), parts along dimension 0, may hold values 0 or 1
Outputs:
- purified: bfloat16 [8192, 1024], P(('snap', 'row'), 'col'), parts along dimension 0
- traces: float32 [4], P('snap'), parts along dimension 0
There are 2 independent parts, one for each index of `snap`. A program takes and returns all parts, laid end to end along the dimension named above; each array names one. Nothing has to cross between parts.
All inputs are finite; a program needn't handle non-finite values. No bound on the sum of `pattern` or of `filter_mask` on one device may be relied on, other than what follows from the above.
Results may differ from a plain program's by a relative error of at most 0.006.
Values may be sent and summed in bfloat16 or wider, within the bound.
A program may use at most 64 MiB of HBM per device.

v0:
```python
import functools

import jax
import jax.numpy as jnp
from jax import lax
from jax.experimental import pallas as pl
from jax.experimental.pallas import tpu as pltpu
from jax.sharding import PartitionSpec as P

BLK = 32
LANE = 128
CHUNKS = 8
LAG = 3
MESH = pl.DeviceIdType.MESH


def expander(width):
    row = lax.broadcasted_iota(jnp.int32, (LANE, width), 0)
    col = lax.broadcasted_iota(jnp.int32, (LANE, width), 1)
    return (col // BLK == row).astype(jnp.bfloat16)


def lanes_padded(value):
    short = LANE - value.shape[1]
    return jnp.concatenate([value, jnp.zeros((value.shape[0], short), value.dtype)], 1)


def valid_slots(first_row, rows, first_slot, half, total):
    row = lax.broadcasted_iota(jnp.int32, (rows, LANE), 0) + first_row
    slot = lax.broadcasted_iota(jnp.int32, (rows, LANE), 1) + first_slot
    column = row + slot - half
    return ((column >= 0) & (column < total)).astype(jnp.float32)


def kernel(
    row_size,
    density_in,
    pattern_in,
    filter_in,
    out,
    traces,
    density,
    pattern,
    filter_mask,
    kept,
    near,
    right,
    total_sum,
    squared,
    keep_filter,
    result,
    part,
    parts,
    send_sem,
    sib_sem,
    p_sem,
    psib_sem,
    q_sem,
    qsib_sem,
    tsend_sem,
    trecv_sem,
    load_sem,
    round_sem,
    done_sem,
):
    rows, width = density_in.shape
    half = width // BLK
    block_rows = rows // BLK
    chunk = rows // CHUNKS
    snap = lax.axis_index("snap")
    me = lax.axis_index("row")
    core = lax.axis_index("col")
    odd = lax.rem(me, 2)
    partner = me + 1 - 2 * odd
    onward = me + 2 - 4 * odd
    origin = me - 2 + 4 * odd
    has_onward = (onward >= 0) & (onward < row_size)
    has_origin = (origin >= 0) & (origin < row_size)
    p_side = 1 - odd
    q_side = odd
    other = 1 - core
    total = row_size * block_rows

    barrier = pltpu.get_barrier_semaphore()

    def greet(row, column, semaphore):
        pl.semaphore_signal(semaphore, inc=1, device_id=(snap, row, column), device_id_type=MESH)

    greet(me, other, barrier)
    greet(partner, core, barrier)

    @pl.when(has_onward)
    def _():
        greet(onward, core, barrier)

    @pl.when(has_origin)
    def _():
        greet(origin, core, barrier)

    beside = has_onward.astype(jnp.int32) + has_origin.astype(jnp.int32)
    loads = [
        pltpu.make_async_copy(source, target, load_sem.at[i])
        for i, (source, target) in enumerate(
            ((density_in, density), (pattern_in, pattern), (filter_in, filter_mask))
        )
    ]
    for load in loads:
        load.start()
    loads[1].wait()
    first_slot = core * half
    keep = lanes_padded(pattern[...]).astype(jnp.float32)
    keep = keep * valid_slots(me * block_rows, block_rows, first_slot, half, total)
    spread = jnp.dot(keep.astype(jnp.bfloat16), expander(width), preferred_element_type=jnp.float32)
    loads[0].wait()
    for m in range(block_rows):
        at = pl.ds(m * BLK, BLK)
        kept[core, at, :] = (
            density[at, :].astype(jnp.float32) * spread[m : m + 1, :]
        ).astype(jnp.bfloat16)
    pl.semaphore_wait(barrier, 2 + beside)

    def block(k):
        return pl.ds(k * chunk, chunk)

    def lanes(k, short):
        above = k * chunk // LANE * LANE
        if short == 0:
            return pl.ds(0, width)
        if short == 1:
            return pl.ds(0, width - above)
        return pl.ds(rows - above - LANE, above + LANE)

    def either(exists, act):
        @pl.when(exists & (core == odd) & (odd == 1))
        def _():
            act(1)

        @pl.when(exists & (core == odd) & (odd == 0))
        def _():
            act(2)

        @pl.when(exists & (core != odd))
        def _():
            act(0)

    def to_partner(k):
        return pltpu.make_async_remote_copy(
            src_ref=kept.at[core, block(k), :],
            dst_ref=near.at[odd, core, block(k), :],
            send_sem=send_sem.at[0, k],
            recv_sem=p_sem.at[k],
            device_id=(snap, partner, core),
            device_id_type=MESH,
        )

    def from_partner(k):
        return pltpu.make_async_remote_copy(
            src_ref=kept.at[core, block(k), :],
            dst_ref=near.at[p_side, core, block(k), :],
            send_sem=send_sem.at[0, k],
            recv_sem=p_sem.at[k],
            device_id=(snap, partner, core),
            device_id_type=MESH,
        )

    def to_onward(k, short):
        return pltpu.make_async_remote_copy(
            src_ref=near.at[p_side, core, block(k), lanes(k, short)],
            dst_ref=near.at[q_side, core, block(k), lanes(k, short)],
            send_sem=send_sem.at[1, k],
            recv_sem=q_sem.at[k],
            device_id=(snap, onward, core),
            device_id_type=MESH,
        )

    def from_origin(k, short):
        return pltpu.make_async_remote_copy(
            src_ref=near.at[p_side, core, block(k), lanes(k, short)],
            dst_ref=near.at[q_side, core, block(k), lanes(k, short)],
            send_sem=send_sem.at[1, k],
            recv_sem=q_sem.at[k],
            device_id=(snap, origin, core),
            device_id_type=MESH,
        )

    def across(side, half_at, k, sent, received):
        return pltpu.make_async_remote_copy(
            src_ref=near.at[side, half_at, block(k), :],
            dst_ref=near.at[side, half_at, block(k), :],
            send_sem=sent,
            recv_sem=received,
            device_id=(snap, me, other),
            device_id_type=MESH,
        )

    own = pltpu.make_async_remote_copy(
        src_ref=kept.at[core],
        dst_ref=kept.at[core],
        send_sem=send_sem.at[4, 0],
        recv_sem=sib_sem,
        device_id=(snap, me, other),
        device_id_type=MESH,
    )
    own_in = pltpu.make_async_remote_copy(
        src_ref=kept.at[other],
        dst_ref=kept.at[other],
        send_sem=send_sem.at[4, 0],
        recv_sem=sib_sem,
        device_id=(snap, me, other),
        device_id_type=MESH,
    )
    own.start()
    for k in range(CHUNKS):
        to_partner(k).start()
    loads[2].wait()
    keep = lanes_padded(filter_mask[...]).astype(jnp.float32)
    keep = keep * valid_slots(me * block_rows, block_rows, 0, half, total)
    keep = pltpu.roll(keep, 0, 1, stride=1, stride_axis=0)
    keep_filter[...] = jnp.dot(
        keep.astype(jnp.bfloat16), expander(3 * width), preferred_element_type=jnp.float32
    )
    right[:, pl.ds(width, 3 * width)] = jnp.zeros((3 * rows, 3 * width), right.dtype)

    own_in.wait_recv()

    def skew(first, second, m, side):
        at = pl.ds(m * BLK, BLK)
        band = jnp.concatenate(
            [first[at, :], second[at, :], jnp.zeros((BLK, LANE), jnp.bfloat16)], 1
        )
        turn = (m * BLK) % LANE
        if turn:
            band = pltpu.roll(band.astype(jnp.float32), turn, 1).astype(jnp.bfloat16)
        to_row = pl.multiple_of(side * rows + m * BLK, BLK)
        to_lane = pl.multiple_of(side * width + m * BLK - turn, LANE)
        right[pl.ds(to_row, BLK), pl.ds(to_lane, 2 * width + LANE)] = band

    for m in range(block_rows):
        skew(kept.at[0], kept.at[1], m, 1)

    @pl.when(jnp.logical_not(has_origin))
    def _():
        near[q_side] = jnp.zeros(near.shape[1:], near.dtype)

    levels = row_size // 2

    def meet(level):
        @pl.when(has_onward)
        def _():
            greet(onward, core, round_sem.at[level])

        @pl.when(has_origin)
        def _():
            greet(origin, core, round_sem.at[level])

    def met(level):
        pl.semaphore_wait(round_sem.at[level], beside)

    def meet_again(level, _):
        meet(level)
        met(level)
        return 0

    step = width // 2

    def own_product(n):
        at = pl.ds(n * step, step)
        total_sum[:, at] = jnp.dot(
            right[pl.ds(rows, rows), pl.ds(2 * width, width)],
            right[pl.ds(rows, rows), pl.ds(width + n * step, step)],
            preferred_element_type=jnp.float32,
        )

    def side_product(side, part_at):
        depth = rows // 2
        from_row = pl.multiple_of(side * rows + part_at * depth, LANE)
        from_lane = pl.multiple_of((1 + side) * width + part_at * depth, LANE)
        to_lane = (side // 2) * width
        for n in range(4):
            at = pl.multiple_of(to_lane + n * step, LANE)
            total_sum[:, pl.ds(at, step)] += jnp.dot(
                right[pl.ds(rows, rows), pl.ds(from_lane, depth)],
                right[pl.ds(from_row, depth), pl.ds(pl.multiple_of(width + at, LANE), step)],
                preferred_element_type=jnp.float32,
            )

    def lay(side, k):
        for m in range(k * chunk // BLK, (k + 1) * chunk // BLK):
            skew(near.at[side, 0], near.at[side, 1], m, 2 * side)

    for k in range(CHUNKS + LAG + 1):
        if k < CHUNKS:
            from_partner(k).wait_recv()
            across(p_side, core, k, send_sem.at[2, k], psib_sem.at[k]).start()

            either(has_onward, lambda short: to_onward(k, short).start())

        if 0 <= k - LAG < CHUNKS:

            either(has_origin, lambda short: from_origin(k - LAG, short).wait_recv())

            @pl.when(has_origin)
            def _():
                across(q_side, core, k - LAG, send_sem.at[3, k - LAG], qsib_sem.at[k - LAG]).start()

        if 1 <= k - 1 < levels:
            met(k - 1)
        if 1 <= k < levels:
            meet(k)
        if k < 6:
            own_product(k)
        late = k - 1
        if 0 <= late < CHUNKS:
            across(p_side, other, late, send_sem.at[2, late], psib_sem.at[late]).wait_recv()
            lay(p_side, late)
            if late == CHUNKS - 1:
                side_product(2 * p_side, 1)
        late = k - 1 - LAG
        if 0 <= late < CHUNKS:

            @pl.when(has_origin)
            def _():
                across(q_side, other, late, send_sem.at[3, late], qsib_sem.at[late]).wait_recv()

            lay(q_side, late)
        if k == max(6, CHUNKS // 2 + 1):
            side_product(2 * p_side, 0)
        if k == max(7, CHUNKS // 2 + 1 + LAG):
            side_product(2 * q_side, 0)
        if k == min(CHUNKS, levels):
            if k < levels:
                met(k)
                lax.fori_loop(k + 1, levels, meet_again, 0)
            greet(partner, core, done_sem)
    side_product(2 * q_side, 1)
    pl.semaphore_wait(done_sem, 1)

    lane = lax.broadcasted_iota(jnp.int32, (LANE, LANE), 1)
    diagonal = lane == lax.broadcasted_iota(jnp.int32, (LANE, LANE), 0)
    kept_sum = jnp.zeros((LANE, LANE), jnp.float32)
    squared_sum = jnp.zeros((LANE, LANE), jnp.float32)
    for b in range(rows // LANE):
        here = pl.ds(width + b * LANE, LANE)
        kept_sum += jnp.where(
            diagonal, right[pl.ds(rows + b * LANE, LANE), pl.ds(2 * width + b * LANE, LANE)].astype(jnp.float32), 0.0
        )
        blocks = []
        for m in range(b * LANE // BLK, (b + 1) * LANE // BLK):
            blocks.append(total_sum[pl.ds(m * BLK, BLK), here] * keep_filter[pl.ds(m, 1), here])
        rounded = jnp.concatenate(blocks, 0).astype(jnp.bfloat16).astype(jnp.float32)
        squared_sum += jnp.where(diagonal, rounded, 0.0)
    part[0] = jnp.sum(kept_sum.reshape(LANE // 8, 8, LANE), 0)
    part[1] = jnp.sum(squared_sum.reshape(LANE // 8, 8, LANE), 0)

    for m in range(block_rows):
        at = pl.ds(m * BLK, BLK)
        squared[at, :] = (total_sum[at, :] * keep_filter[m : m + 1, :]).astype(jnp.bfloat16)

    def share(step_to, _):
        peer = lax.rem(me + step_to, row_size)
        pltpu.make_async_remote_copy(
            src_ref=part,
            dst_ref=parts.at[step_to],
            send_sem=tsend_sem.at[step_to],
            recv_sem=trecv_sem.at[step_to],
            device_id=(snap, peer, core),
            device_id_type=MESH,
        ).start()
        return 0

    lax.fori_loop(1, row_size, share, 0)

    for n in range(4):
        if n < 2:
            column = width + n * step
            place = (1 - core) * width + n * step
            deep = pl.ds(0, 3 * rows)
        else:
            column = 2 * core * width + (n - 2) * step
            place = core * width + (n - 2) * step
            deep = pl.ds(pl.multiple_of(core * rows, LANE), 2 * rows)
        at = pl.ds(pl.multiple_of(column, LANE), step)
        place = pl.ds(pl.multiple_of(place, LANE), step)
        tile = jnp.dot(
            squared[:, deep],
            right[deep, pl.ds(pl.multiple_of(width + column, LANE), step)],
            preferred_element_type=jnp.float32,
        )
        for m in range(block_rows):
            rows_at = pl.ds(m * BLK, BLK)
            result[rows_at, place] = 3.0 * squared[rows_at, at].astype(jnp.float32) - 2.0 * (
                tile[m * BLK : (m + 1) * BLK] * keep_filter[pl.ds(m, 1), at]
            )

    for m in range(block_rows):
        turn = (m * BLK) % LANE
        start = m * BLK - turn
        band = result[pl.ds(m * BLK, BLK), pl.ds(start, width + (LANE if turn else 0))]
        if turn:
            band = pltpu.roll(band, band.shape[1] - turn, 1)
        out[pl.ds(m * BLK, BLK), :] = band[:, :width].astype(jnp.bfloat16)

    def gather(step_to, sums):
        peer = lax.rem(me + row_size - step_to, row_size)
        pltpu.make_async_remote_copy(
            src_ref=part,
            dst_ref=parts.at[step_to],
            send_sem=tsend_sem.at[step_to],
            recv_sem=trecv_sem.at[step_to],
            device_id=(snap, peer, core),
            device_id_type=MESH,
        ).wait()
        return (sums[0] + parts[step_to, 0], sums[1] + parts[step_to, 1])

    sums = lax.fori_loop(1, row_size, gather, (part[0], part[1]))
    traces[0] = jnp.sum(sums[0]) / (total * BLK)
    traces[1] = jnp.sum(sums[1]) / (total * BLK)

    own.wait_send()
    for k in range(CHUNKS):
        to_partner(k).wait_send()
        across(p_side, core, k, send_sem.at[2, k], psib_sem.at[k]).wait_send()

        either(has_onward, lambda short: to_onward(k, short).wait_send())

        @pl.when(has_origin)
        def _():
            across(q_side, core, k, send_sem.at[3, k], qsib_sem.at[k]).wait_send()


def solution(mesh):
    row_size = mesh.shape["row"]

    def per_device(density, pattern, filter_mask):
        rows, width = density.shape
        block_rows = rows // BLK
        return pl.pallas_call(
            functools.partial(kernel, row_size),
            out_shape=(
                pltpu.VMEM((rows, width), jnp.bfloat16),
                jax.ShapeDtypeStruct((2,), jnp.float32),
            ),
            in_specs=[pl.BlockSpec(memory_space=pl.ANY)] * 3,
            out_specs=(
                pl.BlockSpec(memory_space=pltpu.VMEM),
                pl.BlockSpec(memory_space=pltpu.SMEM),
            ),
            scratch_shapes=[
                pltpu.VMEM((rows, width), jnp.bfloat16),
                pltpu.VMEM(pattern.shape, jnp.int32),
                pltpu.VMEM(filter_mask.shape, jnp.int32),
                pltpu.VMEM((2, rows, width), jnp.bfloat16),
                pltpu.VMEM((2, 2, rows, width), jnp.bfloat16),
                pltpu.VMEM((3 * rows, 5 * width), jnp.bfloat16),
                pltpu.VMEM((rows, 3 * width), jnp.float32),
                pltpu.VMEM((rows, 3 * width), jnp.bfloat16),
                pltpu.VMEM((block_rows, 3 * width), jnp.float32),
                pltpu.VMEM((rows, 2 * width), jnp.float32),
                pltpu.VMEM((2, 8, LANE), jnp.float32),
                pltpu.VMEM((row_size, 2, 8, LANE), jnp.float32),
                pltpu.SemaphoreType.DMA((5, CHUNKS)),
                pltpu.SemaphoreType.DMA,
                pltpu.SemaphoreType.DMA((CHUNKS,)),
                pltpu.SemaphoreType.DMA((CHUNKS,)),
                pltpu.SemaphoreType.DMA((CHUNKS,)),
                pltpu.SemaphoreType.DMA((CHUNKS,)),
                pltpu.SemaphoreType.DMA((row_size,)),
                pltpu.SemaphoreType.DMA((row_size,)),
                pltpu.SemaphoreType.DMA((3,)),
                pltpu.SemaphoreType.REGULAR((max(row_size // 2, 1),)),
                pltpu.SemaphoreType.REGULAR,
            ],
            compiler_params=pltpu.CompilerParams(
                collective_id=0, has_side_effects=True, vmem_limit_bytes=56 * 1024 * 1024
            ),
        )(density, pattern, filter_mask)

    return jax.shard_map(
        per_device,
        mesh=mesh,
        in_specs=(P(("snap", "row"), "col"), P(("snap", "row"), "col"), P(("snap", "row"), None)),
        out_specs=(P(("snap", "row"), "col"), P("snap")),
        check_vma=False,
    )
```

profile of v0, /device:TPU:0, one launch (start us, length us, event | category | flops | bytes accessed | tf_op | source)
XLA Modules:
  0.0 29.8 jit_solution(559757458673138678)
XLA Ops:
  0.6 27.9 %shard_map.50 = (bf16[512,512]{1,0:T(8,128)(2,1)S(1)}, f32[2]{0:T(128)}) custom-call(bf16[512,512]{1,0:T(8,128)(2,1)} %density_in.1, s32[16,16]{1,0:T(8,128)} %pattern_in.1, s32[16,32]{1,0:T(8,128)} %filter_in.1), custom_call_target="tpu_custom_call" | custom-call | tf_op jit(solution)/shard_map/pallas_call | solution.py:437
  28.5 0.0 copy-start
  28.5 0.8 %copy.7 = bf16[512,512]{1,0:T(8,128)(2,1)} copy(bf16[512,512]{1,0:T(8,128)(2,1)S(1)} %get-tuple-element.2) | data formatting | bytes 1048576
  29.3 0.0 copy-done
  29.3 0.5 %copy.8 = f32[2]{0:T(128)} copy(f32[2]{0:T(128)S(1)} %copy-done) | data formatting | bytes 16
Async XLA Ops:
  28.5 0.8 %copy-start = (f32[2]{0:T(128)S(1)}, f32[2]{0:T(128)}, u32[]{:S(2)}) copy-start(f32[2]{0:T(128)} %get-tuple-element.7) | copy-start | bytes 28
where the time goes:
time: 30 us; the launch traced here: 29.8 us
  Pallas kernels  27.9 us (93%)
  local copies, waits for them, and re-layouts  1.31 us (4%)
  between operations  0.65 us (2%)
    pallas_call x1, Pallas kernels, per_device(): pl.pallas_call(functools.partial(kernel, row_size), out_shape=(pltpu.VMEM...  27.9 us
    unnamed x4, local copies, waits for them, and re-layouts  1.31 us

commit v1 on v0

v1 whole, which is shorter than its diff:
```python
import functools

import jax
import jax.numpy as jnp
from jax import lax
from jax.experimental import pallas as pl
from jax.experimental.pallas import tpu as pltpu
from jax.sharding import PartitionSpec as P

BLK = 32
LANE = 128
PER = LANE // BLK
MESH = pl.DeviceIdType.MESH

RELAYED = ((1, 0, 4), (3, 0, 2), (3, 2, 2), (2, 0, 2), (2, 2, 2), (0, 0, 4))
DIRECT = (0, 1, 2)
ORDER = (1, 3, 2, 0)


def expander(width):
    row = lax.broadcasted_iota(jnp.int32, (LANE, width), 0)
    col = lax.broadcasted_iota(jnp.int32, (LANE, width), 1)
    return (col // BLK == row).astype(jnp.bfloat16)


def lanes_padded(value):
    short = LANE - value.shape[1]
    return jnp.concatenate([value, jnp.zeros((value.shape[0], short), value.dtype)], 1)


def valid_slots(first_row, rows, first_slot, half, total):
    row = lax.broadcasted_iota(jnp.int32, (rows, LANE), 0) + first_row
    slot = lax.broadcasted_iota(jnp.int32, (rows, LANE), 1) + first_slot
    column = row + slot - half
    return ((column >= 0) & (column < total)).astype(jnp.float32)


def kernel(
    row_size,
    density_in,
    pattern_in,
    filter_in,
    out,
    traces,
    density,
    pattern,
    filter_mask,
    spread,
    kept,
    far,
    opp,
    right,
    total_sum,
    squared,
    keep_filter,
    result,
    outbox,
    part,
    parts,
    load_sem,
    msend_sem,
    xsend_sem,
    m_sem,
    x_sem,
    rsend_sem,
    osend_sem,
    own_sem,
    fsend_sem,
    opp_sem,
    bsend_sem,
    box_sem,
    tsend_sem,
    trecv_sem,
    round_sem,
    done_sem,
):
    rows, width = density_in.shape
    half = width // BLK
    block_rows = rows // BLK
    mine = block_rows // 2
    groups = block_rows // PER
    group = PER * BLK
    tile = mine * BLK
    span = 5 * tile
    snap = lax.axis_index("snap")
    me = lax.axis_index("row")
    core = lax.axis_index("col")
    odd = lax.rem(me, 2)
    other = 1 - core
    partner = me + 1 - 2 * odd
    side = me - 1 + 2 * odd
    onward = me + 2 - 4 * odd
    origin = me - 2 + 4 * odd
    has_onward = (onward >= 0) & (onward < row_size)
    has_origin = (origin >= 0) & (origin < row_size)
    relays = core != odd
    has_far = relays | has_origin
    has_opp = (core == odd) | has_origin
    total = row_size * block_rows

    barrier = pltpu.get_barrier_semaphore()

    def greet(row, column, semaphore):
        pl.semaphore_signal(semaphore, inc=1, device_id=(snap, row, column), device_id_type=MESH)

    greet(me, other, barrier)
    greet(partner, core, barrier)
    greet(partner, other, barrier)

    @pl.when(has_onward)
    def _():
        greet(onward, core, barrier)
        greet(onward, other, barrier)

    @pl.when(has_origin)
    def _():
        greet(origin, core, barrier)
        greet(origin, other, barrier)
        greet(side, other, barrier)

    def band_of(flip, g):
        return pl.ds(pl.multiple_of((g + flip * (groups - 1 - 2 * g)) * group, group), group)

    loads = [pltpu.make_async_copy(pattern_in, pattern, load_sem.at[0])]
    for g in ORDER:
        at = band_of(core, g)
        loads.append(pltpu.make_async_copy(density_in.at[at, :], density.at[at, :], load_sem.at[1 + g]))
    loads.append(pltpu.make_async_copy(filter_in, filter_mask, load_sem.at[1 + groups]))
    for load in loads:
        load.start()

    def window(flip, row, height, slot, slots):
        row = row + flip * (block_rows - height - 2 * row)
        slot = slot + flip * (2 * half - slots - 2 * slot)
        return (
            pl.ds(pl.multiple_of(row * BLK, BLK), height * BLK),
            pl.ds(pl.multiple_of(slot * BLK, LANE), slots * BLK),
        )

    def relayed(flip, k):
        g, row, height = RELAYED[k]
        slots = PER * (g + 1)
        return window(flip, PER * g + row, height, half - slots, slots)

    def direct(flip, k):
        g = DIRECT[k]
        return window(flip, PER * g, PER, 0, half - PER * (g + 1))

    def send_relayed(j, k):
        at = relayed(j, k)
        return pltpu.make_async_remote_copy(
            src_ref=kept.at[at],
            dst_ref=far.at[at],
            send_sem=msend_sem.at[k],
            recv_sem=m_sem.at[j, k],
            device_id=(snap, partner, odd),
            device_id_type=MESH,
        )

    to_row = jnp.where(relays, partner, side)
    to_core = jnp.where(relays, odd, 1 - odd)

    def send_direct(j, k):
        at = direct(j, k)
        return pltpu.make_async_remote_copy(
            src_ref=kept.at[at],
            dst_ref=far.at[at],
            send_sem=xsend_sem.at[k],
            recv_sem=x_sem.at[k],
            device_id=(snap, to_row, to_core),
            device_id_type=MESH,
        )

    def relay(j, k):
        at = relayed(j, k)
        return pltpu.make_async_remote_copy(
            src_ref=far.at[at],
            dst_ref=far.at[at],
            send_sem=rsend_sem.at[j, k],
            recv_sem=m_sem.at[j, k],
            device_id=(snap, onward, odd),
            device_id_type=MESH,
        )

    def own_half(column, g):
        at = (band_of(column, g), pl.ds(pl.multiple_of(column * width, LANE), width))
        return pltpu.make_async_remote_copy(
            src_ref=kept.at[at],
            dst_ref=kept.at[at],
            send_sem=osend_sem.at[g],
            recv_sem=own_sem.at[g],
            device_id=(snap, me, other),
            device_id_type=MESH,
        )

    near_parts = (
        (groups - 2, half - PER, 3 * PER),
        (groups - 1, half - 2 * PER, 3 * PER),
        (groups - 1, half + PER, 3 * PER),
        (groups - 2, half + 2 * PER, 2 * PER),
    )

    def forward(column, n):
        g, slot, slots = near_parts[n]
        at = window(column, PER * g, PER, slot, slots)
        return pltpu.make_async_remote_copy(
            src_ref=far.at[at],
            dst_ref=opp.at[at],
            send_sem=fsend_sem.at[n],
            recv_sem=opp_sem.at[n],
            device_id=(snap, me, other),
            device_id_type=MESH,
        )

    loads[0].wait()
    keep = lanes_padded(pattern[...]).astype(jnp.float32)
    keep = keep * valid_slots(me * block_rows, block_rows, core * half, half, total)
    spread[...] = jnp.dot(keep.astype(jnp.bfloat16), expander(width), preferred_element_type=jnp.float32)
    own_lanes = pl.ds(pl.multiple_of(core * width, LANE), width)
    pieces = {1: (0,), 3: (1, 2), 2: (3, 4), 0: (5,)}
    for n, g in enumerate(ORDER):
        loads[1 + n].wait()
        first = g + core * (groups - 1 - 2 * g)
        for r in range(PER):
            m = first * PER + r
            at = pl.ds(pl.multiple_of(m * BLK, BLK), BLK)
            kept[at, own_lanes] = (density[at, :].astype(jnp.float32) * spread[pl.ds(m, 1), :]).astype(jnp.bfloat16)
        if n == 0:
            beside = 2 * has_onward.astype(jnp.int32) + 3 * has_origin.astype(jnp.int32)
            pl.semaphore_wait(barrier, 3 + beside)
        for k in pieces[g]:
            send_relayed(core, k).start()
        own_half(core, g).start()

    @pl.when(has_far)
    def _():
        for k in range(len(DIRECT)):
            send_direct(core, k).start()

    levels = max(row_size // 2, 1)

    def meet(level):
        @pl.when(has_onward)
        def _():
            greet(onward, core, round_sem.at[level])

        @pl.when(has_origin)
        def _():
            greet(origin, core, round_sem.at[level])

    def met(level):
        pl.semaphore_wait(round_sem.at[level], has_onward.astype(jnp.int32) + has_origin.astype(jnp.int32))

    def round_of(level):
        if 1 <= level - 1 < levels:
            met(level - 1)
        if 1 <= level < levels:
            meet(level)

    round_of(1)
    loads[-1].wait()
    keep = lanes_padded(filter_mask[pl.ds(pl.multiple_of(core * mine, mine), mine), :]).astype(jnp.float32)
    keep = keep * valid_slots(me * block_rows + core * mine, mine, 0, half, total)
    keep = pltpu.roll(keep, 0, 1, stride=1, stride_axis=0)
    keep_filter[...] = jnp.dot(keep.astype(jnp.bfloat16), expander(span), preferred_element_type=jnp.float32)
    right[:, pl.ds(width, span)] = jnp.zeros((span, span), right.dtype)

    def lay(source, first, place):
        for r in range(PER):
            at = pl.ds(pl.multiple_of((first + r) * BLK, BLK), BLK)
            band = jnp.concatenate([source[at, :], jnp.zeros((BLK, LANE), jnp.bfloat16)], 1)
            if r:
                band = pltpu.roll(band.astype(jnp.float32), r * BLK, 1).astype(jnp.bfloat16)
            to = pl.ds(pl.multiple_of((place + r) * BLK, BLK), BLK)
            right[to, pl.ds(pl.multiple_of(place * BLK, LANE), 2 * width + LANE)] = band

    def lay_own(g):
        first = (g + other * (groups - 1 - 2 * g)) * PER
        lay(kept, first, 2 * mine - core * mine + first)

    def lay_far(g):
        first = (g + core * (groups - 1 - 2 * g)) * PER
        lay(far, first, first + core * 3 * mine)

    def lay_opp(g):
        first = (g + other * (groups - 1 - 2 * g)) * PER
        lay(opp, first, first + other * 4 * mine - core * mine)

    def tiles(first, count):
        first = first + core * (5 - count - 2 * first)
        return pl.multiple_of(first * tile, tile)

    def product(k, depth, first, count, add):
        here = tiles(k, depth)
        there = tiles(first, count)
        value = jnp.dot(
            right[pl.ds(2 * tile, tile), pl.ds(pl.multiple_of(width + here, LANE), depth * tile)],
            right[pl.ds(here, depth * tile), pl.ds(pl.multiple_of(width + there, LANE), count * tile)],
            preferred_element_type=jnp.float32,
        )
        if add:
            total_sum[:, pl.ds(there, count * tile)] += value
        else:
            total_sum[:, pl.ds(there, count * tile)] = value

    def arrive(k):
        @pl.when(has_far)
        def _():
            for j in range(2):
                relay(j, k).wait_recv()

        @pl.when(relays & has_onward)
        def _():
            for j in range(2):
                relay(j, k).start()

    def pass_on(n):
        @pl.when(has_far)
        def _():
            forward(core, n).start()

    def arrive_direct(k):
        @pl.when(has_far)
        def _():
            send_direct(other, k).wait_recv()

    for g in ORDER:
        own_half(other, g).wait_recv()
        lay_own(g)
    arrive(0)
    round_of(2)
    product(2, 2, 0, 5, False)
    arrive(1)
    arrive(2)
    round_of(3)
    arrive(3)
    arrive(4)
    pass_on(0)
    round_of(4)
    arrive(5)
    pass_on(1)

    @pl.when(has_far)
    def _():
        lay_far(0)

    for level in range(5, min(levels, 6) + 1):
        round_of(level)
    if levels > 5:

        def again(level, _):
            met(level - 1)
            meet(level)
            return 0

        lax.fori_loop(7, levels, again, 0)
        met(levels - 1)
    greet(me, other, done_sem)
    greet(partner, core, done_sem)
    greet(partner, other, done_sem)

    arrive_direct(0)
    pass_on(2)

    @pl.when(has_far)
    def _():
        lay_far(3)

    arrive_direct(1)
    pass_on(3)

    @pl.when(has_far)
    def _():
        lay_far(2)
        product(1, 1, 0, 4, True)

    def take_far():
        @pl.when(has_far)
        def _():
            send_direct(other, 2).wait_recv()
            lay_far(1)
            product(0, 1, 0, 3, True)

    def take_opp():
        @pl.when(has_opp)
        def _():
            for n in (1, 2):
                forward(other, n).wait_recv()
            lay_opp(groups - 1)
            for n in (0, 3):
                forward(other, n).wait_recv()
            lay_opp(groups - 2)
            product(4, 1, 2, 3, True)

    @pl.when(relays)
    def _():
        take_far()
        take_opp()

    @pl.when(core == odd)
    def _():
        take_opp()
        take_far()

    pl.semaphore_wait(done_sem, 3)

    lane = lax.broadcasted_iota(jnp.int32, (LANE, LANE), 1)
    diagonal = lane == lax.broadcasted_iota(jnp.int32, (LANE, LANE), 0)
    kept_sum = jnp.zeros((LANE, LANE), jnp.float32)
    squared_sum = jnp.zeros((LANE, LANE), jnp.float32)
    for b in range(tile // LANE):
        here = pl.ds(2 * tile + b * LANE, LANE)
        kept_sum += jnp.where(diagonal, right[here, pl.ds(width + 2 * tile + b * LANE, LANE)].astype(jnp.float32), 0.0)
        blocks = []
        for m in range(b * PER, (b + 1) * PER):
            blocks.append(total_sum[pl.ds(m * BLK, BLK), here] * keep_filter[pl.ds(m, 1), here])
        squared_sum += jnp.where(diagonal, jnp.concatenate(blocks, 0).astype(jnp.bfloat16).astype(jnp.float32), 0.0)
    part[0] = jnp.sum(kept_sum.reshape(LANE // 8, 8, LANE), 0)
    part[1] = jnp.sum(squared_sum.reshape(LANE // 8, 8, LANE), 0)

    number = 2 * me + core

    def share(step, peer):
        return pltpu.make_async_remote_copy(
            src_ref=part,
            dst_ref=parts.at[step],
            send_sem=tsend_sem.at[step],
            recv_sem=trecv_sem.at[step],
            device_id=(snap, peer // 2, lax.rem(peer, 2)),
            device_id_type=MESH,
        )

    def give(step, _):
        share(step, lax.rem(number + step, 2 * row_size)).start()
        return 0

    lax.fori_loop(1, 2 * row_size, give, 0)

    for m in range(mine):
        at = pl.ds(m * BLK, BLK)
        squared[at, :] = (total_sum[at, :] * keep_filter[m : m + 1, :]).astype(jnp.bfloat16)

    def cube(first, low, depth):
        there = pl.ds(tiles(first, 1), tile)
        here = pl.ds(tiles(low, depth), depth * tile)
        value = jnp.dot(
            squared[:, here],
            right[here, pl.ds(pl.multiple_of(width + tiles(first, 1), LANE), tile)],
            preferred_element_type=jnp.float32,
        )
        for m in range(mine):
            at = pl.ds(m * BLK, BLK)
            result[at, there] = 3.0 * squared[at, there].astype(jnp.float32) - 2.0 * (
                value[m * BLK : (m + 1) * BLK] * keep_filter[pl.ds(m, 1), there]
            )

    def unskewed(m, column):
        turn = (m % PER) * BLK
        start = pl.multiple_of(column * width + m * BLK - turn, LANE)
        band = result[pl.ds(m * BLK, BLK), pl.ds(start, width + (LANE if turn else 0))]
        if turn:
            band = pltpu.roll(band, band.shape[1] - turn, 1)
        return band[:, :width].astype(jnp.bfloat16)

    def box(column, n):
        here = pl.ds(n * group, group)
        there = pl.ds(pl.multiple_of(column * tile + n * group, group), group)
        return pltpu.make_async_remote_copy(
            src_ref=outbox.at[here, :],
            dst_ref=out.at[there, :],
            send_sem=bsend_sem.at[n],
            recv_sem=box_sem.at[n],
            device_id=(snap, me, other),
            device_id_type=MESH,
        )

    cube(4, 2, 3)
    cube(3, 1, 4)
    cube(2, 0, 5)
    for m in range(mine):
        outbox[pl.ds(m * BLK, BLK), :] = unskewed(m, other)
        if m % PER == PER - 1:
            box(core, m // PER).start()
    cube(1, 0, 4)
    cube(0, 0, 3)
    for m in range(mine):
        at = pl.ds(pl.multiple_of(core * tile + m * BLK, BLK), BLK)
        out[at, :] = unskewed(m, core)

    def gather(step, sums):
        share(step, lax.rem(number + 2 * row_size - step, 2 * row_size)).wait()
        return (sums[0] + parts[step, 0], sums[1] + parts[step, 1])

    sums = lax.fori_loop(1, 2 * row_size, gather, (part[0], part[1]))
    traces[0] = jnp.sum(sums[0]) / (total * BLK)
    traces[1] = jnp.sum(sums[1]) / (total * BLK)

    for n in range(tile // group):
        box(core, n).wait_send()
        box(other, n).wait_recv()
    for g in range(groups):
        own_half(core, g).wait_send()
    for k in range(len(RELAYED)):
        send_relayed(core, k).wait_send()

        @pl.when(relays & has_onward)
        def _():
            for j in range(2):
                relay(j, k).wait_send()

    @pl.when(has_far)
    def _():
        for k in range(len(DIRECT)):
            send_direct(core, k).wait_send()
        for n in range(len(near_parts)):
            forward(core, n).wait_send()


def solution(mesh):
    row_size = mesh.shape["row"]

    def per_device(density, pattern, filter_mask):
        rows, width = density.shape
        block_rows = rows // BLK
        tile = rows // 2
        span = 5 * tile
        dma = pltpu.SemaphoreType.DMA
        return pl.pallas_call(
            functools.partial(kernel, row_size),
            out_shape=(
                pltpu.VMEM((rows, width), jnp.bfloat16),
                jax.ShapeDtypeStruct((2,), jnp.float32),
            ),
            in_specs=[pl.BlockSpec(memory_space=pl.ANY)] * 3,
            out_specs=(
                pl.BlockSpec(memory_space=pltpu.VMEM),
                pl.BlockSpec(memory_space=pltpu.SMEM),
            ),
            scratch_shapes=[
                pltpu.VMEM((rows, width), jnp.bfloat16),
                pltpu.VMEM(pattern.shape, jnp.int32),
                pltpu.VMEM(filter_mask.shape, jnp.int32),
                pltpu.VMEM((block_rows, width), jnp.float32),
                pltpu.VMEM((rows, 2 * width), jnp.bfloat16),
                pltpu.VMEM((rows, 2 * width), jnp.bfloat16),
                pltpu.VMEM((rows, 2 * width), jnp.bfloat16),
                pltpu.VMEM((span, span + 2 * width), jnp.bfloat16),
                pltpu.VMEM((tile, span), jnp.float32),
                pltpu.VMEM((tile, span), jnp.bfloat16),
                pltpu.VMEM((block_rows // 2, span), jnp.float32),
                pltpu.VMEM((tile, span), jnp.float32),
                pltpu.VMEM((tile, width), jnp.bfloat16),
                pltpu.VMEM((2, 8, LANE), jnp.float32),
                pltpu.VMEM((2 * row_size, 2, 8, LANE), jnp.float32),
                dma((2 + block_rows // PER,)),
                dma((len(RELAYED),)),
                dma((len(DIRECT),)),
                dma((2, len(RELAYED))),
                dma((len(DIRECT),)),
                dma((2, len(RELAYED))),
                dma((block_rows // PER,)),
                dma((block_rows // PER,)),
                dma((4,)),
                dma((4,)),
                dma((2,)),
                dma((2,)),
                dma((2 * row_size,)),
                dma((2 * row_size,)),
                pltpu.SemaphoreType.REGULAR((max(row_size // 2, 1),)),
                pltpu.SemaphoreType.REGULAR,
            ],
            compiler_params=pltpu.CompilerParams(
                collective_id=0, has_side_effects=True, vmem_limit_bytes=56 * 1024 * 1024
            ),
        )(density, pattern, filter_mask)

    return jax.shard_map(
        per_device,
        mesh=mesh,
        in_specs=(P(("snap", "row"), "col"), P(("snap", "row"), "col"), P(("snap", "row"), None)),
        out_specs=(P(("snap", "row"), "col"), P("snap")),
        check_vma=False,
    )
```

time: 30 us -> 28.7 us (0.957)
  Pallas kernels: 27.9 us -> 26.5 us
    pallas_call x1, Pallas kernels: 27.9 us -> 26.5 us  [per_device(): pl.pallas_call(functools.partial(kernel, row_size), out_shape=(pltpu.VMEM...]
where the time goes in v1:
time: 28.7 us; the launch traced here: 28.4 us
  Pallas kernels  26.5 us (92%)
  local copies, waits for them, and re-layouts  1.31 us (5%)
  between operations  0.65 us (2%)
    pallas_call x1, Pallas kernels, per_device(): pl.pallas_call(functools.partial(kernel, row_size), out_shape=(pltpu.VMEM...  26.5 us
    unnamed x4, local copies, waits for them, and re-layouts  1.31 us

profile of v1, /device:TPU:0, one launch (start us, length us, event | category | flops | bytes accessed | tf_op | source)
XLA Modules:
  0.0 28.4 jit_solution(13511306225980988831)
XLA Ops:
  0.6 26.5 %shard_map.50 = (bf16[512,512]{1,0:T(8,128)(2,1)S(1)}, f32[2]{0:T(128)}) custom-call(bf16[512,512]{1,0:T(8,128)(2,1)} %density_in.1, s32[16,16]{1,0:T(8,128)} %pattern_in.1, s32[16,32]{1,0:T(8,128)} %filter_in.1), custom_call_target="tpu_custom_call" | custom-call | tf_op jit(solution)/shard_map/pallas_call | solution.py:528
  27.1 0.0 copy-start
  27.1 0.8 %copy.7 = bf16[512,512]{1,0:T(8,128)(2,1)} copy(bf16[512,512]{1,0:T(8,128)(2,1)S(1)} %get-tuple-element.2) | data formatting | bytes 1048576
  27.9 0.0 copy-done
  27.9 0.5 %copy.8 = f32[2]{0:T(128)} copy(f32[2]{0:T(128)S(1)} %copy-done) | data formatting | bytes 16
Async XLA Ops:
  27.1 0.8 %copy-start = (f32[2]{0:T(128)S(1)}, f32[2]{0:T(128)}, u32[]{:S(2)}) copy-start(f32[2]{0:T(128)} %get-tuple-element.7) | copy-start | bytes 28
